TPU v7x, 32 devices: a whole 2x2x4 slice. The times are simulated.
32 devices in a mesh: orient: 8 (over z, y), dom: 4 (over x, core).
Axes of the slice: x: 2, y: 2, z: 4, core: 2. Of those that a mesh axis runs over, the one named last changes fastest.
Arguments:
- particles: bfloat16 [256, 8448], P(('dom', 'orient')), parts along dimension 0, may hold values from -12 to 12
- defocus: float32 [256], P(('dom', 'orient')), parts along dimension 0, may hold values from 10 to 60
- inv_noise: float32 [4224], replicated, may hold values from 0.5 to 2
- references: bfloat16 [13824, 8448], P(('dom', 'orient')), parts along dimension 0, may hold values from -0.25 to 0.25
- thresholds: int32 [256], P('dom'), parts along dimension 0, may hold values from 512 to 1023
- range_start: int32 [256], P('dom'), parts along dimension 0, may hold values from 0 to 3455
- range_len: int32 [256], P('dom'), parts along dimension 0, may hold values from 36 to 1727
Outputs:
- posterior: float32 [256, 3456], P('dom', 'orient'), parts along dimension 0
- cumulative: float32 [256, 3456], P('dom', 'orient'), parts along dimension 0
- log_evidence: float32 [256], P('dom'), parts along dimension 0
- kept_mass: float32 [256], P('dom'), parts along dimension 0
There are 4 independent parts, one for each index of `dom`. A program takes and returns all parts, laid end to end along the dimension named above; an argument that names none is the same for every part. Nothing has to cross between parts.
All inputs are finite; a program needn't handle non-finite values.
Results may differ from a plain program's by a relative error of at most 0.0004.
The roundings to bfloat16 on the way count: a program that leaves them out, or rounds other values in their place, can miss the bound.
Values may be sent and summed in bfloat16 or wider, within the bound.
A program may use at most 64 MiB of HBM per device.

v0:
```python
import functools
import math

import jax
import jax.numpy as jnp
from jax import lax
from jax.experimental import pallas as pl
from jax.experimental.pallas import tpu as pltpu
from jax.sharding import PartitionSpec as P

MESH = pl.DeviceIdType.MESH
DIMS = (((1,), (1,)), ((), ()))
PIECES = 3
SPANS = ((0, 4), (4, 6))
ROWS = 16


def sin_of(x):
    k = jnp.floor(x * (1.0 / math.pi) + 0.5)
    r = x - k * 3.140625
    r = r - k * 9.67502593994140625e-4
    r = r - k * 1.509957990978376432e-7
    s = r * r
    p = jnp.float32(-2.3889859e-8)
    p = p * s + 2.7525562e-6
    p = p * s - 1.9840874e-4
    p = p * s + 8.3333310e-3
    p = p * s - 1.6666667e-1
    y = r + r * s * p
    half = k * 0.5
    return jnp.where(half == jnp.floor(half), y, -y)


def loop(count, body):
    if count <= 4:
        for i in range(count):
            body(i)
    else:
        def step(i, carry):
            body(i)
            return carry
        lax.fori_loop(0, count, step, 0)


def kernel(
    n, particles, defocus, noise_hbm, references, starts_hbm, lens_hbm,
    expon_hbm, prefix_hbm, sgath,
    gath, dgath, refs, ctf, ctf_power, power, weighted, acc, mine, expon, prefix, noise, starts, lens,
    own_sem, ref_sem, up_send, down_send, side_send, recv, dup_send, ddown_send, dside_send, d_recv, s_send, s_recv,
):
    wide = 2
    deep = n // wide
    per = particles.shape[0]
    feat = particles.shape[1]
    coef = feat // 2
    size = coef // PIECES
    ori = references.shape[0]
    total_ori = n * ori
    parts = n * per
    group = wide * per
    me = lax.axis_index("orient")
    row = lax.div(me, wide)
    col = lax.rem(me, wide)
    partner = row * wide + (1 - col)
    has_up = row + 1 < deep
    has_down = row > 0

    def cut(c):
        return pl.ds(c * size, size)

    def span(c):
        return pl.ds(SPANS[c][0] * size, (SPANS[c][1] - SPANS[c][0]) * size)

    def peer(t):
        return lax.rem(me + t, n)

    def near(act):
        act(partner)

        @pl.when(has_up)
        def _():
            act(me + wide)

        @pl.when(has_down)
        def _():
            act(me - wide)

    barrier = pltpu.get_barrier_semaphore()

    def greet(target):
        pl.semaphore_signal(barrier, inc=1, device_id={"orient": target}, device_id_type=MESH)

    near(greet)
    order = list(range(len(SPANS)))
    paired = -1
    pieces = [c for k in range(PIECES) for c in (k, k + PIECES)]
    own = pltpu.make_async_copy(particles, gath.at[me], own_sem.at[0])
    own.start()
    own_d = pltpu.make_async_copy(defocus, dgath.at[me], own_sem.at[1])
    own_d.start()
    loads = {}
    for c in pieces:
        loads[c] = pltpu.make_async_copy(references.at[:, cut(c)], refs.at[:, cut(c)], ref_sem.at[c])
        loads[c].start()
    small = [
        pltpu.make_async_copy(noise_hbm, noise, own_sem.at[2]),
        pltpu.make_async_copy(starts_hbm, starts, own_sem.at[3]),
        pltpu.make_async_copy(lens_hbm, lens, own_sem.at[4]),
    ]
    for copy in small:
        copy.start()
    own.wait()
    own_d.wait()
    pl.semaphore_wait(barrier, 1 + has_up.astype(jnp.int32) + has_down.astype(jnp.int32))

    def remote(block, send_sem, recv_sem, target):
        return pltpu.make_async_remote_copy(
            src_ref=block, dst_ref=block, send_sem=send_sem, recv_sem=recv_sem,
            device_id={"orient": target}, device_id_type=MESH)

    def up(c, source):
        if c is None:
            return remote(dgath.at[source], dup_send.at[source], d_recv.at[source], me + wide)
        return remote(gath.at[source, :, span(c)], up_send.at[c, source], recv.at[c, source], me + wide)

    def down(c, source):
        if c is None:
            return remote(dgath.at[source], ddown_send.at[source], d_recv.at[source], me - wide)
        return remote(gath.at[source, :, span(c)], down_send.at[c, source], recv.at[c, source], me - wide)

    def side(c, source):
        if c is None:
            return remote(dgath.at[source], dside_send.at[source], d_recv.at[source], partner)
        return remote(gath.at[source, :, span(c)], side_send.at[c, source], recv.at[c, source], partner)

    def s_copy(source, target):
        return pltpu.make_async_remote_copy(
            src_ref=mine, dst_ref=sgath.at[source],
            send_sem=s_send.at[target], recv_sem=s_recv.at[source],
            device_id={"orient": target}, device_id_type=MESH)

    def both(c, source):
        @pl.when(has_up)
        def _():
            up(c, source).start()

        @pl.when(has_down)
        def _():
            down(c, source).start()

    side(None, me).start()
    both(None, me)
    for c in order:
        side(c, me).start()
    for c in order:
        both(c, me)

    def handle(c, t):
        @pl.when(row >= t)
        def _():
            for column in (col, 1 - col) if c == paired else (col,):
                source = (row - t) * wide + column
                side(c, source).wait_recv()

                @pl.when(has_up)
                def _():
                    up(c, source).start()

                if c != paired:
                    side(c, source).start()

        @pl.when(row + t < deep)
        def _():
            for column in (col, 1 - col) if c == paired else (col,):
                source = (row + t) * wide + column
                side(c, source).wait_recv()

                @pl.when(has_down)
                def _():
                    down(c, source).start()

                if c != paired:
                    side(c, source).start()

    def arrived(c):
        if c != paired:
            for r in range(deep):
                side(c, r * wide + 1 - col).wait_recv()

    eye8 = lax.broadcasted_iota(jnp.int32, (per, per), 0) == lax.broadcasted_iota(jnp.int32, (per, per), 1)

    def ctf_row(r, wait=True):
        if wait:
            side(None, r * wide + 1 - col).wait_recv()
        columns = []
        for j in range(wide):
            columns.append(jnp.sum(jnp.where(eye8, dgath[r * wide + j], 0.0), axis=1, keepdims=True))
        d = jnp.concatenate(columns, axis=0)
        rows = pl.ds(pl.multiple_of(r * group, group), group)

        def body(k):
            index = k * size + lax.broadcasted_iota(jnp.int32, (1, size), 1)
            row_pos = lax.shift_right_logical(index, 7).astype(jnp.float32)
            col_pos = ((index & 127) - 64).astype(jnp.float32)
            freq = math.pi * (row_pos * row_pos + col_pos * col_pos) / 16384.0
            value = -sin_of(d * freq + 0.07)
            ctf[rows, cut(k)] = value
            ctf_power[rows, cut(k)] = (value * value * noise[cut(k)].reshape(1, size)).astype(jnp.bfloat16)

        for k in range(PIECES):
            body(k)

    def ctf_rows(t):
        @pl.when(row >= t)
        def _():
            ctf_row(row - t)

        @pl.when(row + t < deep)
        def _():
            ctf_row(row + t)

    def power_piece(k):
        loads[k].wait()
        loads[k + PIECES].wait()

        def body(i):
            rows = pl.ds(pl.multiple_of(i * ROWS, ROWS), ROWS)
            re = refs[rows, cut(k)].astype(jnp.float32)
            im = refs[rows, cut(k + PIECES)].astype(jnp.float32)
            power[rows, cut(k)] = (re * re + im * im).astype(jnp.bfloat16)

        loop(ori // ROWS, body)

    def energy_piece(k):
        term = -0.5 * lax.dot_general(
            ctf_power[:, cut(k)], power[:, cut(k)], DIMS, preferred_element_type=jnp.float32)
        if k == 0:
            acc[...] = term
        else:
            acc[...] += term

    def cross_piece(c):
        k = c % PIECES

        def body(i):
            rows = pl.ds(pl.multiple_of(i * group, group), group)
            block = gath[pl.ds(i * wide, wide), :, cut(c)].astype(jnp.float32).reshape(group, size)
            weighted[rows, :] = (block * ctf[rows, cut(k)] * noise[cut(k)].reshape(1, size)).astype(jnp.bfloat16)

        loop(deep, body)
        acc[...] += lax.dot_general(weighted[...], refs[:, cut(c)], DIMS, preferred_element_type=jnp.float32)

    short = deep == 4
    power_piece(0)
    power_piece(1)
    for copy in small:
        copy.wait()
    if short:
        tasks = {
            (1, 0): [lambda: ctf_row(row)],
            (1, 1): [lambda: power_piece(2), lambda: ctf_rows(1)],
            (2, 1): [lambda: ctf_rows(2)],
            (3, 0): [lambda: ctf_rows(3), lambda: energy_piece(0)],
            (3, 1): [lambda: energy_piece(1), lambda: energy_piece(2)],
        }
    else:
        tasks = {(1, 0): [lambda: power_piece(2)]}
    for t in range(1, deep):
        handle(None, t)
        for i, c in enumerate(order):
            handle(c, t)
            for task in tasks.get((t, i), ()):
                task()
    if not short:
        for r in range(deep):
            side(None, r * wide + 1 - col).wait_recv()
        loop(deep, lambda r: ctf_row(r, wait=False))
        for k in range(PIECES):
            energy_piece(k)
    for c in order:
        arrived(c)
        for piece in range(*SPANS[c]):
            cross_piece(piece)

    scores = acc[...]
    top = jnp.max(scores, axis=1, keepdims=True)
    e = jnp.exp(scores - top)
    expon[:, :ori] = e
    eye = lax.broadcasted_iota(jnp.int32, (parts, parts), 0) == lax.broadcasted_iota(jnp.int32, (parts, parts), 1)

    def to_col(x):
        return jnp.sum(jnp.where(eye, x, 0), axis=1, keepdims=True)

    def to_row(x):
        return jnp.sum(jnp.where(eye, x, 0.0), axis=0, keepdims=True)

    start = to_col(starts[...])
    length = to_col(lens[...])
    ids = me * ori + lax.broadcasted_iota(jnp.int32, (parts, ori), 1)
    rel = ids - start
    inside = jnp.where(rel < 0, rel + total_ori, rel) < length
    first = me * ori - start
    first_inside = jnp.where(first < 0, first + total_ori, first) < length
    in_range = jnp.sum(jnp.where(inside, e, 0.0), axis=1, keepdims=True)
    ahead = jnp.sum(jnp.where(rel < 0, e, 0.0), axis=1, keepdims=True)
    ahead = jnp.where(first_inside, 0.0, ahead)
    for i, value in enumerate((top, jnp.sum(e, axis=1, keepdims=True), in_range, ahead)):
        line = to_row(value)
        mine[i : i + 1, :] = line
        sgath[me, i : i + 1, :] = line
    for t in range(1, n):
        s_copy(me, peer(t)).start()

    lanes = 128
    blocks = expon.shape[1] // lanes
    if ori < expon.shape[1]:
        expon[:, ori:] = jnp.zeros((parts, expon.shape[1] - ori), jnp.float32)
    upper = (
        lax.broadcasted_iota(jnp.int32, (lanes, lanes), 0) <= lax.broadcasted_iota(jnp.int32, (lanes, lanes), 1)
    ).astype(jnp.bfloat16)
    carry = jnp.zeros((parts, 1), jnp.float32)
    for b in range(blocks):
        x = expon[:, b * lanes : (b + 1) * lanes]
        high = x.astype(jnp.bfloat16)
        rest = x - high.astype(jnp.float32)
        mid = rest.astype(jnp.bfloat16)
        low = (rest - mid.astype(jnp.float32)).astype(jnp.bfloat16)
        run = carry
        for piece in (low, mid, high):
            run = run + jnp.dot(piece, upper, preferred_element_type=jnp.float32)
        prefix[:, b * lanes : (b + 1) * lanes] = run
        carry = run[:, lanes - 1 : lanes]

    outs = [
        pltpu.make_async_copy(expon, expon_hbm, own_sem.at[0]),
        pltpu.make_async_copy(prefix, prefix_hbm, own_sem.at[1]),
    ]
    for copy in outs:
        copy.start()

    def drain(c, source, along, across):
        if along:
            @pl.when(has_up & (lax.div(source, wide) <= row))
            def _():
                up(c, source).wait_send()

            @pl.when(has_down & (lax.div(source, wide) >= row))
            def _():
                down(c, source).wait_send()

        if across:
            side(c, source).wait_send()

    for c in [None] + order:
        for r in range(deep):
            drain(c, r * wide + col, True, c != paired)
            if c == paired:
                drain(c, r * wide + 1 - col, True, False)
    for t in range(1, n):
        s_copy(me, peer(t)).wait_send()
    for copy in outs:
        copy.wait()
    for t in range(1, n):
        s_copy(peer(t), me).wait_recv()


def finish(n, expon, prefix, sgath, thresholds, posterior, cumulative, evidence, kept_mass):
    parts, ori = posterior.shape
    me = lax.axis_index("orient")
    eye = lax.broadcasted_iota(jnp.int32, (parts, parts), 0) == lax.broadcasted_iota(jnp.int32, (parts, parts), 1)

    def to_col(x):
        return jnp.sum(jnp.where(eye, x, 0), axis=1, keepdims=True)

    stats = [sgath[s] for s in range(n)]
    best = stats[0][0:1]
    for s in stats[1:]:
        best = jnp.maximum(best, s[0:1])
    scale = [jnp.exp(s[0:1] - best) for s in stats]
    base = jnp.zeros_like(best)
    my_base = base
    bases = []
    for s in range(n):
        my_base = jnp.where(me == s, base, my_base)
        bases.append(base)
        base = base + scale[s] * stats[s][1:2]
    total = base
    limit = thresholds[...].astype(jnp.float32) / 1024.0 * total
    kept = jnp.zeros_like(best)
    for s in range(n):
        left = limit - bases[s] - scale[s] * stats[s][3:4]
        kept = kept + jnp.minimum(jnp.maximum(left, 0.0), scale[s] * stats[s][2:3])
    kept_mass[...] = kept / total
    evidence[...] = best + jnp.log(total)
    my_scale = to_col(jnp.exp(sgath[me, 0:1, :] - best) / total)
    my_base = to_col(my_base / total)
    posterior[...] = expon[:, :ori] * my_scale
    cumulative[...] = my_base + prefix[:, :ori] * my_scale


def on_device(n, particles, defocus, inv_noise, references, thresholds, range_start, range_len):
    per, feat = particles.shape
    coef = feat // 2
    ori = references.shape[0]
    parts = n * per
    padded = -(-ori // 128) * 128
    chunks = 2 * PIECES
    f32, bf16 = jnp.float32, jnp.bfloat16
    vmem = pl.BlockSpec(memory_space=pltpu.VMEM)
    hbm = pl.BlockSpec(memory_space=pl.ANY)
    dma = pltpu.SemaphoreType.DMA
    expon, prefix, stats = pl.pallas_call(
        functools.partial(kernel, n),
        out_shape=(
            jax.ShapeDtypeStruct((parts, padded), f32),
            jax.ShapeDtypeStruct((parts, padded), f32),
            jax.ShapeDtypeStruct((n, 4, parts), f32),
        ),
        in_specs=[hbm] * 6,
        out_specs=[hbm, hbm, vmem],
        scratch_shapes=[
            pltpu.VMEM((n, per, feat), bf16),
            pltpu.VMEM((n, 1, per), f32),
            pltpu.VMEM((ori, feat), bf16),
            pltpu.VMEM((parts, coef), f32),
            pltpu.VMEM((parts, coef), bf16),
            pltpu.VMEM((ori, coef), bf16),
            pltpu.VMEM((parts, coef // PIECES), bf16),
            pltpu.VMEM((parts, ori), f32),
            pltpu.VMEM((4, parts), f32),
            pltpu.VMEM((parts, padded), f32),
            pltpu.VMEM((parts, padded), f32),
            pltpu.VMEM((coef,), f32),
            pltpu.VMEM((1, parts), jnp.int32),
            pltpu.VMEM((1, parts), jnp.int32),
            dma((5,)),
            dma((chunks,)),
            dma((len(SPANS), n)),
            dma((len(SPANS), n)),
            dma((len(SPANS), n)),
            dma((len(SPANS), n)),
            dma((n,)),
            dma((n,)),
            dma((n,)),
            dma((n,)),
            dma((n,)),
            dma((n,)),
        ],
        compiler_params=pltpu.CompilerParams(
            collective_id=0, has_side_effects=True, vmem_limit_bytes=56 * 1024 * 1024
        ),
    )(
        particles, defocus.reshape(1, per), inv_noise, references,
        range_start.reshape(1, parts), range_len.reshape(1, parts),
    )
    outs = pl.pallas_call(
        functools.partial(finish, n),
        out_shape=(
            jax.ShapeDtypeStruct((parts, ori), f32),
            jax.ShapeDtypeStruct((parts, ori), f32),
            jax.ShapeDtypeStruct((1, parts), f32),
            jax.ShapeDtypeStruct((1, parts), f32),
        ),
        in_specs=[vmem] * 4,
        out_specs=[vmem] * 4,
    )(expon, prefix, stats, thresholds.reshape(1, parts))
    return outs[0], outs[1], outs[2].reshape(parts), outs[3].reshape(parts)


def solution(mesh):
    return jax.shard_map(
        functools.partial(on_device, mesh.shape["orient"]),
        mesh=mesh,
        in_specs=(
            P(("dom", "orient"), None),
            P(("dom", "orient")),
            P(),
            P(("dom", "orient"), None),
            P("dom"),
            P("dom"),
            P("dom"),
        ),
        out_specs=(P("dom", "orient"), P("dom", "orient"), P("dom"), P("dom")),
        check_vma=False,
    )
```

profile of v0, /device:TPU:0, one launch (start us, length us, event | category | flops | bytes accessed | tf_op | source)
XLA Modules:
  0.0 30.0 jit_solution(4804940652004812125)
XLA Ops:
  0.6 27.6 %shard_map.102 = (f32[64,512]{1,0:T(8,128)}, f32[64,512]{1,0:T(8,128)}, f32[8,4,64]{2,1,0:T(4,128)}) custom-call(bf16[8,8448]{1,0:T(8,128)(2,1)} %particles.1, f32[1,8]{1,0:T(1,128)} %bitcast.6, f32[4224]{0:T(1024)} %noise_hbm.1, bf16[432,8448]{1,0:T(8,128)(2,1)} %references.1, s32[1,64]{1,0:T(1,128)} %bitcast.7, s32[1,64]{1,0:T(1,128)} %bitcast.8), custom_call_target="tpu_custom_call" | custom-call | tf_op jit(solution)/shard_map/pallas_call | solution.py:412
  28.2 1.8 %shard_map.103 = (f32[64,432]{1,0:T(8,128)}, f32[64,432]{1,0:T(8,128)}, f32[1,64]{1,0:T(1,128)}, f32[1,64]{1,0:T(1,128)}) custom-call(f32[64,512]{1,0:T(8,128)} %get-tuple-element.11.expon, f32[64,512]{1,0:T(8,128)} %get-tuple-element.12.prefix, f32[8,4,64]{2,1,0:T(4,128)} %get-tuple-element.13.sgath, s32[1,64]{1,0:T(1,128)} %bitcast.9), custom_call_target="tpu_custom_call" | custom-call | tf_op jit(solution)/shard_map/pallas_call | solution.py:456
where the time goes:
time: 30.2 us; the launch traced here: 30 us
  Pallas kernels  29.4 us (97%)
  between operations  0.64 us (2%)
    pallas_call x1, Pallas kernels, on_device(): pl.pallas_call(functools.partial(kernel, n), out_shape=(jax.ShapeDtypeStr...  27.6 us
    pallas_call x1, Pallas kernels, on_device(): pl.pallas_call(functools.partial(finish, n), out_shape=(jax.ShapeDtypeStr...  1.79 us

commit v1 on v0

--- a/solution.py
+++ b/solution.py
@@ -44,8 +44,8 @@
 
 def kernel(
     n, particles, defocus, noise_hbm, references, starts_hbm, lens_hbm,
-    expon_hbm, prefix_hbm, sgath,
-    gath, dgath, refs, ctf, ctf_power, power, weighted, acc, mine, expon, prefix, noise, starts, lens,
+    expon, prefix, sgath,
+    gath, dgath, refs, ctf, ctf_power, power, weighted, acc, mine, noise, starts, lens,
     own_sem, ref_sem, up_send, down_send, side_send, recv, dup_send, ddown_send, dside_send, d_recv, s_send, s_recv,
 ):
     wide = 2
@@ -331,13 +331,6 @@
         prefix[:, b * lanes : (b + 1) * lanes] = run
         carry = run[:, lanes - 1 : lanes]
 
-    outs = [
-        pltpu.make_async_copy(expon, expon_hbm, own_sem.at[0]),
-        pltpu.make_async_copy(prefix, prefix_hbm, own_sem.at[1]),
-    ]
-    for copy in outs:
-        copy.start()
-
     def drain(c, source, along, across):
         if along:
             @pl.when(has_up & (lax.div(source, wide) <= row))
@@ -358,8 +351,6 @@
                 drain(c, r * wide + 1 - col, True, False)
     for t in range(1, n):
         s_copy(me, peer(t)).wait_send()
-    for copy in outs:
-        copy.wait()
     for t in range(1, n):
         s_copy(peer(t), me).wait_recv()
 
@@ -412,12 +403,12 @@
     expon, prefix, stats = pl.pallas_call(
         functools.partial(kernel, n),
         out_shape=(
-            jax.ShapeDtypeStruct((parts, padded), f32),
-            jax.ShapeDtypeStruct((parts, padded), f32),
-            jax.ShapeDtypeStruct((n, 4, parts), f32),
+            pltpu.VMEM((parts, padded), f32),
+            pltpu.VMEM((parts, padded), f32),
+            pltpu.VMEM((n, 4, parts), f32),
         ),
         in_specs=[hbm] * 6,
-        out_specs=[hbm, hbm, vmem],
+        out_specs=[vmem] * 3,
         scratch_shapes=[
             pltpu.VMEM((n, per, feat), bf16),
             pltpu.VMEM((n, 1, per), f32),
@@ -428,8 +419,6 @@
             pltpu.VMEM((parts, coef // PIECES), bf16),
             pltpu.VMEM((parts, ori), f32),
             pltpu.VMEM((4, parts), f32),
-            pltpu.VMEM((parts, padded), f32),
-            pltpu.VMEM((parts, padded), f32),
             pltpu.VMEM((coef,), f32),
             pltpu.VMEM((1, parts), jnp.int32),
             pltpu.VMEM((1, parts), jnp.int32),
@@ -447,12 +436,13 @@
             dma((n,)),
         ],
         compiler_params=pltpu.CompilerParams(
-            collective_id=0, has_side_effects=True, vmem_limit_bytes=56 * 1024 * 1024
+            collective_id=0, has_side_effects=True, vmem_limit_bytes=48 * 1024 * 1024
         ),
-    )(
-        particles, defocus.reshape(1, per), inv_noise, references,
-        range_start.reshape(1, parts), range_len.reshape(1, parts),
-    )
+    )(*(
+        pltpu.with_memory_space_constraint(x, pltpu.HBM) for x in (
+            particles, defocus.reshape(1, per), inv_noise, references,
+            range_start.reshape(1, parts), range_len.reshape(1, parts))
+    ))
     outs = pl.pallas_call(
         functools.partial(finish, n),
         out_shape=(
@@ -463,6 +453,7 @@
         ),
         in_specs=[vmem] * 4,
         out_specs=[vmem] * 4,
+        compiler_params=pltpu.CompilerParams(vmem_limit_bytes=8 * 1024 * 1024),
     )(expon, prefix, stats, thresholds.reshape(1, parts))
     return outs[0], outs[1], outs[2].reshape(parts), outs[3].reshape(parts)
 

time: 30.2 us -> 28.6 us (0.947)
  Pallas kernels: 29.4 us -> 27.8 us
    pallas_call x1, Pallas kernels: 1.79 us -> 0.82 us  [on_device(): pl.pallas_call(functools.partial(finish, n), out_shape=(jax.ShapeDtypeStr...]
    pallas_call x1, Pallas kernels: 27.6 us -> 27 us  [on_device(): pl.pallas_call(functools.partial(kernel, n), out_shape=(pltpu.VMEM((parts...]
where the time goes in v1:
time: 28.6 us; the launch traced here: 28.5 us
  Pallas kernels  27.8 us (97%)
  between operations  0.66 us (2%)
    pallas_call x1, Pallas kernels, on_device(): pl.pallas_call(functools.partial(kernel, n), out_shape=(pltpu.VMEM((parts...  27 us
    pallas_call x1, Pallas kernels, on_device(): pl.pallas_call(functools.partial(finish, n), out_shape=(jax.ShapeDtypeStr...  0.82 us

profile of v1, /device:TPU:0, one launch (start us, length us, event | category | flops | bytes accessed | tf_op | source)
XLA Modules:
  0.0 28.5 jit_solution(2143740499554666238)
XLA Ops:
  0.6 0.0 copy-start
  0.6 27.0 %shard_map.102 = (f32[64,512]{1,0:T(8,128)S(1)}, f32[64,512]{1,0:T(8,128)S(1)}, f32[8,4,64]{2,1,0:T(4,128)S(1)}) custom-call(bf16[8,8448]{1,0:T(8,128)(2,1)} %particles.1, f32[1,8]{1,0:T(1,128)} %bitcast.7, f32[4224]{0:T(1024)} %noise_hbm.1, bf16[432,8448]{1,0:T(8,128)(2,1)} %references.1, s32[1,64]{1,0:T(1,128)} %bitcast.8, s32[1,64]{1,0:T(1,128)} %bitcast.9), custom_call_target="tpu_custom_call" | custom-call | tf_op jit(solution)/shard_map/pallas_call | solution.py:403
  27.6 0.0 copy-done
  27.7 0.8 %shard_map.103 = (f32[64,432]{1,0:T(8,128)}, f32[64,432]{1,0:T(8,128)}, f32[1,64]{1,0:T(1,128)}, f32[1,64]{1,0:T(1,128)}) custom-call(f32[64,512]{1,0:T(8,128)S(1)} %get-tuple-element.11.expon, f32[64,512]{1,0:T(8,128)S(1)} %get-tuple-element.12.prefix, f32[8,4,64]{2,1,0:T(4,128)S(1)} %get-tuple-element.13.sgath, s32[1,64]{1,0:T(1,128)S(1)} %bitcast.6), custom_call_target="tpu_custom_call" | custom-call | tf_op jit(solution)/shard_map/pallas_call | solution.py:446
Async XLA Ops:
  0.6 27.0 %copy-start = (s32[64]{0:T(128)S(1)}, s32[64]{0:T(128)}, u32[]{:S(2)}) copy-start(s32[64]{0:T(128)} %param.11) | copy-start | bytes 772

commit v2 on v1

--- a/solution.py
+++ b/solution.py
@@ -12,6 +12,7 @@
 DIMS = (((1,), (1,)), ((), ()))
 PIECES = 3
 SPANS = ((0, 4), (4, 6))
+ORDER = tuple(c for k in range(PIECES) for c in (k, k + PIECES))
 ROWS = 16
 
 
@@ -46,7 +47,8 @@
     n, particles, defocus, noise_hbm, references, starts_hbm, lens_hbm,
     expon, prefix, sgath,
     gath, dgath, refs, ctf, ctf_power, power, weighted, acc, mine, noise, starts, lens,
-    own_sem, ref_sem, up_send, down_send, side_send, recv, dup_send, ddown_send, dside_send, d_recv, s_send, s_recv,
+    own_sem, piece_sem, ref_sem, up_send, down_send, side_send, recv, side_recv,
+    dup_send, ddown_send, beside_send, beside_recv, pair_recv, far_send, far_recv, s_send, s_recv,
 ):
     wide = 2
     deep = n // wide
@@ -68,8 +70,12 @@
     def cut(c):
         return pl.ds(c * size, size)
 
+    short = deep == 4
+    spans = [(c, c + 1) for c in ORDER] if short else SPANS
+    lowest, highest = row == 0, row == deep - 1
+
     def span(c):
-        return pl.ds(SPANS[c][0] * size, (SPANS[c][1] - SPANS[c][0]) * size)
+        return pl.ds(spans[c][0] * size, (spans[c][1] - spans[c][0]) * size)
 
     def peer(t):
         return lax.rem(me + t, n)
@@ -91,17 +97,23 @@
         pl.semaphore_signal(barrier, inc=1, device_id={"orient": target}, device_id_type=MESH)
 
     near(greet)
-    order = list(range(len(SPANS)))
-    paired = -1
-    pieces = [c for k in range(PIECES) for c in (k, k + PIECES)]
-    own = pltpu.make_async_copy(particles, gath.at[me], own_sem.at[0])
-    own.start()
+    if short:
+        @pl.when(lowest)
+        def _():
+            for column in range(wide):
+                greet((deep - 1) * wide + column)
+
+    order = list(range(len(spans)))
+    own = [
+        pltpu.make_async_copy(particles.at[:, span(c)], gath.at[me, :, span(c)], piece_sem.at[c])
+        for c in order
+    ]
     own_d = pltpu.make_async_copy(defocus, dgath.at[me], own_sem.at[1])
     own_d.start()
-    loads = {}
-    for c in pieces:
-        loads[c] = pltpu.make_async_copy(references.at[:, cut(c)], refs.at[:, cut(c)], ref_sem.at[c])
-        loads[c].start()
+    for copy in own:
+        copy.start()
+    for c in ORDER:
+        pltpu.make_async_copy(references.at[:, cut(c)], refs.at[:, cut(c)], ref_sem.at[c % PIECES]).start()
     small = [
         pltpu.make_async_copy(noise_hbm, noise, own_sem.at[2]),
         pltpu.make_async_copy(starts_hbm, starts, own_sem.at[3]),
@@ -109,35 +121,47 @@
     ]
     for copy in small:
         copy.start()
-    own.wait()
     own_d.wait()
-    pl.semaphore_wait(barrier, 1 + has_up.astype(jnp.int32) + has_down.astype(jnp.int32))
+    greeted = 1 + has_up.astype(jnp.int32) + has_down.astype(jnp.int32)
+    if short:
+        greeted = greeted + wide * highest.astype(jnp.int32)
+    pl.semaphore_wait(barrier, greeted)
 
     def remote(block, send_sem, recv_sem, target):
         return pltpu.make_async_remote_copy(
             src_ref=block, dst_ref=block, send_sem=send_sem, recv_sem=recv_sem,
             device_id={"orient": target}, device_id_type=MESH)
 
+    def block(c, source):
+        return gath.at[source, :, span(c)]
+
     def up(c, source):
-        if c is None:
-            return remote(dgath.at[source], dup_send.at[source], d_recv.at[source], me + wide)
-        return remote(gath.at[source, :, span(c)], up_send.at[c, source], recv.at[c, source], me + wide)
+        return remote(block(c, source), up_send, recv.at[c, lax.div(source, wide)], me + wide)
 
     def down(c, source):
-        if c is None:
-            return remote(dgath.at[source], ddown_send.at[source], d_recv.at[source], me - wide)
-        return remote(gath.at[source, :, span(c)], down_send.at[c, source], recv.at[c, source], me - wide)
+        return remote(block(c, source), down_send, recv.at[c, lax.div(source, wide)], me - wide)
 
     def side(c, source):
-        if c is None:
-            return remote(dgath.at[source], dside_send.at[source], d_recv.at[source], partner)
-        return remote(gath.at[source, :, span(c)], side_send.at[c, source], recv.at[c, source], partner)
+        return remote(block(c, source), side_send, side_recv.at[c], partner)
+
+    def beside(source):
+        return remote(dgath.at[source], beside_send, beside_recv, partner)
+
+    def pair(r):
+        return dgath.at[pl.ds(r * wide, wide)]
+
+    def pair_up(r):
+        return remote(pair(r), dup_send, pair_recv.at[r], me + wide)
+
+    def pair_down(r):
+        return remote(pair(r), ddown_send, pair_recv.at[r], me - wide)
 
     def s_copy(source, target):
         return pltpu.make_async_remote_copy(
-            src_ref=mine, dst_ref=sgath.at[source],
-            send_sem=s_send.at[target], recv_sem=s_recv.at[source],
+            src_ref=mine, dst_ref=sgath.at[source], send_sem=s_send, recv_sem=s_recv,
             device_id={"orient": target}, device_id_type=MESH)
+
+    others = sgath.at[pl.ds(0, n - 1)]
 
     def both(c, source):
         @pl.when(has_up)
@@ -148,50 +172,90 @@
         def _():
             down(c, source).start()
 
-    side(None, me).start()
-    both(None, me)
+    def far(column):
+        return remote(dgath.at[me], far_send, far_recv.at[col], column)
+
+    far_both = remote(pair(deep - 1), far_send, far_recv.at[0], partner)
+
+    if short:
+        @pl.when(highest)
+        def _():
+            for column in range(wide):
+                far(column).start()
+
+    beside(me).start()
     for c in order:
+        own[c].wait()
         side(c, me).start()
-    for c in order:
         both(c, me)
+
+    def relay_pairs(t):
+        if t == 0:
+            beside(partner).wait_recv()
+
+            @pl.when(has_up)
+            def _():
+                pair_up(row).start()
+
+            @pl.when(has_down)
+            def _():
+                pair_down(row).start()
+
+            return
+
+        @pl.when(row >= t)
+        def _():
+            pair_up(row - t).wait_recv()
+
+            @pl.when(has_up)
+            def _():
+                pair_up(row - t).start()
+
+        direct = short and t == deep - 1
+
+        @pl.when(row + t < deep)
+        def _():
+            if direct:
+                for column in range(wide):
+                    source = (deep - 1) * wide + column
+                    remote(dgath.at[source], far_send, far_recv.at[column], partner).wait_recv()
+            else:
+                pair_down(row + t).wait_recv()
+
+                @pl.when(has_down & (row > 1 if short and t == deep - 2 else True))
+                def _():
+                    pair_down(row + t).start()
 
     def handle(c, t):
         @pl.when(row >= t)
         def _():
-            for column in (col, 1 - col) if c == paired else (col,):
-                source = (row - t) * wide + column
-                side(c, source).wait_recv()
-
-                @pl.when(has_up)
-                def _():
-                    up(c, source).start()
-
-                if c != paired:
-                    side(c, source).start()
+            source = (row - t) * wide + col
+            up(c, source).wait_recv()
+
+            @pl.when(has_up)
+            def _():
+                up(c, source).start()
+
+            side(c, source).start()
 
         @pl.when(row + t < deep)
         def _():
-            for column in (col, 1 - col) if c == paired else (col,):
-                source = (row + t) * wide + column
-                side(c, source).wait_recv()
-
-                @pl.when(has_down)
-                def _():
-                    down(c, source).start()
-
-                if c != paired:
-                    side(c, source).start()
+            source = (row + t) * wide + col
+            down(c, source).wait_recv()
+
+            @pl.when(has_down)
+            def _():
+                down(c, source).start()
+
+            side(c, source).start()
 
     def arrived(c):
-        if c != paired:
-            for r in range(deep):
-                side(c, r * wide + 1 - col).wait_recv()
+        blocks = gath.at[pl.ds(0, deep), :, span(c)]
+        remote(blocks, side_send, side_recv.at[c], partner).wait_recv()
 
     eye8 = lax.broadcasted_iota(jnp.int32, (per, per), 0) == lax.broadcasted_iota(jnp.int32, (per, per), 1)
 
-    def ctf_row(r, wait=True):
-        if wait:
-            side(None, r * wide + 1 - col).wait_recv()
+    def ctf_row(r):
         columns = []
         for j in range(wide):
             columns.append(jnp.sum(jnp.where(eye8, dgath[r * wide + j], 0.0), axis=1, keepdims=True))
@@ -220,8 +284,8 @@
             ctf_row(row + t)
 
     def power_piece(k):
-        loads[k].wait()
-        loads[k + PIECES].wait()
+        both_parts = pl.ds(0, 2 * size)
+        pltpu.make_async_copy(references.at[:, both_parts], refs.at[:, both_parts], ref_sem.at[k]).wait()
 
         def body(i):
             rows = pl.ds(pl.multiple_of(i * ROWS, ROWS), ROWS)
@@ -250,36 +314,40 @@
         loop(deep, body)
         acc[...] += lax.dot_general(weighted[...], refs[:, cut(c)], DIMS, preferred_element_type=jnp.float32)
 
-    short = deep == 4
     power_piece(0)
     power_piece(1)
     for copy in small:
         copy.wait()
     if short:
         tasks = {
-            (1, 0): [lambda: ctf_row(row)],
-            (1, 1): [lambda: power_piece(2), lambda: ctf_rows(1)],
-            (2, 1): [lambda: ctf_rows(2)],
-            (3, 0): [lambda: ctf_rows(3), lambda: energy_piece(0)],
-            (3, 1): [lambda: energy_piece(1), lambda: energy_piece(2)],
+            (1, 0): [lambda: power_piece(2)],
+            (1, 1): [lambda: ctf_row(row)],
+            (1, 5): [lambda: relay_pairs(1)],
+            (2, 0): [lambda: ctf_rows(1)],
+            (2, 3): [lambda: relay_pairs(2)],
+            (2, 4): [lambda: ctf_rows(2)],
+            (3, 1): [lambda: relay_pairs(3), lambda: ctf_rows(3)],
+            (3, 2): [lambda: energy_piece(0)],
+            (3, 3): [lambda: energy_piece(1)],
+            (3, 4): [lambda: energy_piece(2)],
         }
     else:
         tasks = {(1, 0): [lambda: power_piece(2)]}
+    relay_pairs(0)
     for t in range(1, deep):
-        handle(None, t)
-        for i, c in enumerate(order):
+        if not short:
+            relay_pairs(t)
+        for c in order:
             handle(c, t)
-            for task in tasks.get((t, i), ()):
+            for task in tasks.get((t, c), ()):
                 task()
     if not short:
-        for r in range(deep):
-            side(None, r * wide + 1 - col).wait_recv()
-        loop(deep, lambda r: ctf_row(r, wait=False))
+        loop(deep, ctf_row)
         for k in range(PIECES):
             energy_piece(k)
     for c in order:
         arrived(c)
-        for piece in range(*SPANS[c]):
+        for piece in range(*spans[c]):
             cross_piece(piece)
 
     scores = acc[...]
@@ -331,28 +399,29 @@
         prefix[:, b * lanes : (b + 1) * lanes] = run
         carry = run[:, lanes - 1 : lanes]
 
-    def drain(c, source, along, across):
-        if along:
-            @pl.when(has_up & (lax.div(source, wide) <= row))
-            def _():
-                up(c, source).wait_send()
-
-            @pl.when(has_down & (lax.div(source, wide) >= row))
-            def _():
-                down(c, source).wait_send()
-
-        if across:
-            side(c, source).wait_send()
-
-    for c in [None] + order:
-        for r in range(deep):
-            drain(c, r * wide + col, True, c != paired)
-            if c == paired:
-                drain(c, r * wide + 1 - col, True, False)
-    for t in range(1, n):
-        s_copy(me, peer(t)).wait_send()
-    for t in range(1, n):
-        s_copy(peer(t), me).wait_recv()
+    def sent(blocks, pairs, send_sem, pair_sem):
+        remote(gath.at[pl.ds(0, blocks)], send_sem, side_recv.at[0], partner).wait_send()
+        remote(dgath.at[pl.ds(0, pairs * wide)], pair_sem, beside_recv, partner).wait_send()
+
+    beside(me).wait_send()
+    remote(gath.at[pl.ds(0, deep)], side_send, side_recv.at[0], partner).wait_send()
+    for r in range(deep - 1):
+        @pl.when(row == r)
+        def _():
+            sent(r + 1, r + 1, up_send, dup_send)
+
+        @pl.when(row == deep - 1 - r)
+        def _():
+            skipped = short and r == deep - 2
+            sent(r + 1, r if skipped else r + 1, down_send, ddown_send)
+
+    if short:
+        @pl.when(highest)
+        def _():
+            far_both.wait_send()
+
+    remote(others, s_send, s_recv, partner).wait_send()
+    remote(others, s_send, s_recv, partner).wait_recv()
 
 
 def finish(n, expon, prefix, sgath, thresholds, posterior, cumulative, evidence, kept_mass):
@@ -424,16 +493,15 @@
             pltpu.VMEM((1, parts), jnp.int32),
             dma((5,)),
             dma((chunks,)),
-            dma((len(SPANS), n)),
-            dma((len(SPANS), n)),
-            dma((len(SPANS), n)),
-            dma((len(SPANS), n)),
-            dma((n,)),
-            dma((n,)),
-            dma((n,)),
-            dma((n,)),
-            dma((n,)),
-            dma((n,)),
+            dma((PIECES,)),
+            dma, dma, dma,
+            dma((chunks, n // 2)),
+            dma((chunks,)),
+            dma, dma, dma, dma,
+            dma((n // 2,)),
+            dma,
+            dma((2,)),
+            dma, dma,
         ],
         compiler_params=pltpu.CompilerParams(
             collective_id=0, has_side_effects=True, vmem_limit_bytes=48 * 1024 * 1024

time: 28.6 us -> 26.6 us (0.930)
  Pallas kernels: 27.8 us -> 25.8 us
    pallas_call x1, Pallas kernels: 27 us -> 25 us  [on_device(): pl.pallas_call(functools.partial(kernel, n), out_shape=(pltpu.VMEM((parts...]
where the time goes in v2:
time: 26.6 us; the launch traced here: 26.5 us
  Pallas kernels  25.8 us (97%)
  between operations  0.66 us (2%)
    pallas_call x1, Pallas kernels, on_device(): pl.pallas_call(functools.partial(kernel, n), out_shape=(pltpu.VMEM((parts...  25 us
    pallas_call x1, Pallas kernels, on_device(): pl.pallas_call(functools.partial(finish, n), out_shape=(jax.ShapeDtypeStr...  0.82 us

profile of v2, /device:TPU:0, one launch (start us, length us, event | category | flops | bytes accessed | tf_op | source)
XLA Modules:
  0.0 26.5 jit_solution(9044918520978262873)
XLA Ops:
  0.6 0.0 copy-start
  0.6 25.0 %shard_map.102 = (f32[64,512]{1,0:T(8,128)S(1)}, f32[64,512]{1,0:T(8,128)S(1)}, f32[8,4,64]{2,1,0:T(4,128)S(1)}) custom-call(bf16[8,8448]{1,0:T(8,128)(2,1)} %particles.1, f32[1,8]{1,0:T(1,128)} %bitcast.7, f32[4224]{0:T(1024)} %noise_hbm.1, bf16[432,8448]{1,0:T(8,128)(2,1)} %references.1, s32[1,64]{1,0:T(1,128)} %bitcast.8, s32[1,64]{1,0:T(1,128)} %bitcast.9), custom_call_target="tpu_custom_call" | custom-call | tf_op jit(solution)/shard_map/pallas_call | solution.py:472
  25.6 0.0 copy-done
  25.6 0.8 %shard_map.103 = (f32[64,432]{1,0:T(8,128)}, f32[64,432]{1,0:T(8,128)}, f32[1,64]{1,0:T(1,128)}, f32[1,64]{1,0:T(1,128)}) custom-call(f32[64,512]{1,0:T(8,128)S(1)} %get-tuple-element.11.expon, f32[64,512]{1,0:T(8,128)S(1)} %get-tuple-element.12.prefix, f32[8,4,64]{2,1,0:T(4,128)S(1)} %get-tuple-element.13.sgath, s32[1,64]{1,0:T(1,128)S(1)} %bitcast.6), custom_call_target="tpu_custom_call" | custom-call | tf_op jit(solution)/shard_map/pallas_call | solution.py:514
Async XLA Ops:
  0.6 25.0 %copy-start = (s32[64]{0:T(128)S(1)}, s32[64]{0:T(128)}, u32[]{:S(2)}) copy-start(s32[64]{0:T(128)} %param.11) | copy-start | bytes 772

commit v3 on v2

--- a/solution.py
+++ b/solution.py
@@ -12,6 +12,8 @@
 DIMS = (((1,), (1,)), ((), ()))
 PIECES = 3
 SPANS = ((0, 4), (4, 6))
+EARLY = 1
+STEPS = ((0,), (1, 2), (3, 4, 5))
 ORDER = tuple(c for k in range(PIECES) for c in (k, k + PIECES))
 ROWS = 16
 
@@ -104,24 +106,21 @@
                 greet((deep - 1) * wide + column)
 
     order = list(range(len(spans)))
-    own = [
-        pltpu.make_async_copy(particles.at[:, span(c)], gath.at[me, :, span(c)], piece_sem.at[c])
-        for c in order
-    ]
-    own_d = pltpu.make_async_copy(defocus, dgath.at[me], own_sem.at[1])
+    own = pltpu.make_async_copy(particles, gath.at[me], piece_sem)
+    own_d = pltpu.make_async_copy(defocus, dgath.at[me], own_sem.at[0])
     own_d.start()
-    for copy in own:
-        copy.start()
-    for c in ORDER:
-        pltpu.make_async_copy(references.at[:, cut(c)], refs.at[:, cut(c)], ref_sem.at[c % PIECES]).start()
+    own.start()
     small = [
-        pltpu.make_async_copy(noise_hbm, noise, own_sem.at[2]),
-        pltpu.make_async_copy(starts_hbm, starts, own_sem.at[3]),
-        pltpu.make_async_copy(lens_hbm, lens, own_sem.at[4]),
+        pltpu.make_async_copy(noise_hbm, noise, own_sem.at[1]),
+        pltpu.make_async_copy(starts_hbm, starts, own_sem.at[2]),
+        pltpu.make_async_copy(lens_hbm, lens, own_sem.at[3]),
     ]
     for copy in small:
         copy.start()
     own_d.wait()
+    own.wait()
+    for c in ORDER:
+        pltpu.make_async_copy(references.at[:, cut(c)], refs.at[:, cut(c)], ref_sem.at[c % PIECES]).start()
     greeted = 1 + has_up.astype(jnp.int32) + has_down.astype(jnp.int32)
     if short:
         greeted = greeted + wide * highest.astype(jnp.int32)
@@ -139,7 +138,7 @@
         return remote(block(c, source), up_send, recv.at[c, lax.div(source, wide)], me + wide)
 
     def down(c, source):
-        return remote(block(c, source), down_send, recv.at[c, lax.div(source, wide)], me - wide)
+        return remote(block(c, source), down_send, recv.at[c, lax.div(source, wide) - 1], me - wide)
 
     def side(c, source):
         return remote(block(c, source), side_send, side_recv.at[c], partner)
@@ -154,7 +153,7 @@
         return remote(pair(r), dup_send, pair_recv.at[r], me + wide)
 
     def pair_down(r):
-        return remote(pair(r), ddown_send, pair_recv.at[r], me - wide)
+        return remote(pair(r), ddown_send, pair_recv.at[r - 1], me - wide)
 
     def s_copy(source, target):
         return pltpu.make_async_remote_copy(
@@ -175,7 +174,6 @@
     def far(column):
         return remote(dgath.at[me], far_send, far_recv.at[col], column)
 
-    far_both = remote(pair(deep - 1), far_send, far_recv.at[0], partner)
 
     if short:
         @pl.when(highest)
@@ -185,7 +183,6 @@
 
     beside(me).start()
     for c in order:
-        own[c].wait()
         side(c, me).start()
         both(c, me)
 
@@ -226,7 +223,7 @@
                 def _():
                     pair_down(row + t).start()
 
-    def handle(c, t):
+    def rise(c, t):
         @pl.when(row >= t)
         def _():
             source = (row - t) * wide + col
@@ -238,6 +235,7 @@
 
             side(c, source).start()
 
+    def fall(c, t):
         @pl.when(row + t < deep)
         def _():
             source = (row + t) * wide + col
@@ -248,6 +246,10 @@
                 down(c, source).start()
 
             side(c, source).start()
+
+    def handle(c, t):
+        rise(c, t)
+        fall(c, t)
 
     def arrived(c):
         blocks = gath.at[pl.ds(0, deep), :, span(c)]
@@ -295,60 +297,105 @@
 
         loop(ori // ROWS, body)
 
-    def energy_piece(k):
-        term = -0.5 * lax.dot_general(
-            ctf_power[:, cut(k)], power[:, cut(k)], DIMS, preferred_element_type=jnp.float32)
-        if k == 0:
-            acc[...] = term
-        else:
-            acc[...] += term
-
-    def cross_piece(c):
-        k = c % PIECES
-
-        def body(i):
-            rows = pl.ds(pl.multiple_of(i * group, group), group)
-            block = gath[pl.ds(i * wide, wide), :, cut(c)].astype(jnp.float32).reshape(group, size)
-            weighted[rows, :] = (block * ctf[rows, cut(k)] * noise[cut(k)].reshape(1, size)).astype(jnp.bfloat16)
-
-        loop(deep, body)
-        acc[...] += lax.dot_general(weighted[...], refs[:, cut(c)], DIMS, preferred_element_type=jnp.float32)
-
-    power_piece(0)
-    power_piece(1)
+    def energy():
+        total = 0.0
+        for k in range(PIECES):
+            total = total + lax.dot_general(
+                ctf_power[:, cut(k)], power[:, cut(k)], DIMS, preferred_element_type=jnp.float32)
+        acc[...] = -0.5 * total
+
+    def cross(pieces):
+        total = acc[...]
+        for c in pieces:
+            k = c % PIECES
+
+            def body(i):
+                rows = pl.ds(pl.multiple_of(i * group, group), group)
+                raw = gath[pl.ds(i * wide, wide), :, cut(c)].astype(jnp.float32).reshape(group, size)
+                weighted[rows, cut(c)] = (raw * ctf[rows, cut(k)] * noise[cut(k)].reshape(1, size)).astype(jnp.bfloat16)
+
+            loop(deep, body)
+            total = total + lax.dot_general(
+                weighted[:, cut(c)], refs[:, cut(c)], DIMS, preferred_element_type=jnp.float32)
+        acc[...] = total
+
+    for k in range(PIECES):
+        power_piece(k)
+        if k == EARLY:
+            relay_pairs(0)
     for copy in small:
         copy.wait()
     if short:
-        tasks = {
-            (1, 0): [lambda: power_piece(2)],
-            (1, 1): [lambda: ctf_row(row)],
-            (1, 5): [lambda: relay_pairs(1)],
-            (2, 0): [lambda: ctf_rows(1)],
-            (2, 3): [lambda: relay_pairs(2)],
-            (2, 4): [lambda: ctf_rows(2)],
-            (3, 1): [lambda: relay_pairs(3), lambda: ctf_rows(3)],
-            (3, 2): [lambda: energy_piece(0)],
-            (3, 3): [lambda: energy_piece(1)],
-            (3, 4): [lambda: energy_piece(2)],
-        }
+        middle = has_up & has_down
+        for c in order + [len(order)]:
+            if c < len(order):
+                rise(c, 1)
+            if c > 0:
+                fall(c - 1, 1)
+
+        ctf_row(row)
+
+        @pl.when(middle)
+        def _():
+            relay_pairs(1)
+
+
+        @pl.when(lowest)
+        def _():
+            relay_pairs(1)
+            ctf_row(row + 1)
+
+        @pl.when(highest)
+        def _():
+            relay_pairs(1)
+            ctf_row(row - 1)
+
+        for c in order:
+            handle(c, 2)
+            if c == 3:
+                @pl.when(row == deep - 2)
+                def _():
+                    relay_pairs(2)
+
+        @pl.when(row != deep - 2)
+        def _():
+            relay_pairs(2)
+
+        @pl.when(middle)
+        def _():
+            ctf_row(row - 1)
+            ctf_row(row + 1)
+            ctf_rows(2)
+
+        @pl.when(lowest)
+        def _():
+            ctf_rows(2)
+            relay_pairs(3)
+            ctf_rows(3)
+
+        for c in order:
+            handle(c, 3)
+            if c == 1:
+                @pl.when(highest)
+                def _():
+                    ctf_rows(2)
+
+            if c == 3:
+                @pl.when(highest)
+                def _():
+                    relay_pairs(3)
+                    ctf_rows(3)
     else:
-        tasks = {(1, 0): [lambda: power_piece(2)]}
-    relay_pairs(0)
-    for t in range(1, deep):
-        if not short:
+        for t in range(1, deep):
             relay_pairs(t)
-        for c in order:
-            handle(c, t)
-            for task in tasks.get((t, c), ()):
-                task()
-    if not short:
+            for c in order:
+                handle(c, t)
         loop(deep, ctf_row)
-        for k in range(PIECES):
-            energy_piece(k)
-    for c in order:
-        arrived(c)
-        for piece in range(*spans[c]):
-            cross_piece(piece)
+    energy()
+    for step in STEPS if short else [(c,) for c in order]:
+        for c in step:
+            arrived(c)
+        cross([piece for c in step for piece in range(*spans[c])])
 
     scores = acc[...]
     top = jnp.max(scores, axis=1, keepdims=True)
@@ -418,7 +465,7 @@
     if short:
         @pl.when(highest)
         def _():
-            far_both.wait_send()
+            remote(pair(deep - 1), far_send, far_recv.at[0], partner).wait_send()
 
     remote(others, s_send, s_recv, partner).wait_send()
     remote(others, s_send, s_recv, partner).wait_recv()
@@ -485,20 +532,20 @@
             pltpu.VMEM((parts, coef), f32),
             pltpu.VMEM((parts, coef), bf16),
             pltpu.VMEM((ori, coef), bf16),
-            pltpu.VMEM((parts, coef // PIECES), bf16),
+            pltpu.VMEM((parts, feat), bf16),
             pltpu.VMEM((parts, ori), f32),
             pltpu.VMEM((4, parts), f32),
             pltpu.VMEM((coef,), f32),
             pltpu.VMEM((1, parts), jnp.int32),
             pltpu.VMEM((1, parts), jnp.int32),
-            dma((5,)),
-            dma((chunks,)),
+            dma((4,)),
+            dma,
             dma((PIECES,)),
             dma, dma, dma,
-            dma((chunks, n // 2)),
+            dma((chunks, n // 2 - 1)),
             dma((chunks,)),
             dma, dma, dma, dma,
-            dma((n // 2,)),
+            dma((n // 2 - 1,)),
             dma,
             dma((2,)),
             dma, dma,

time: 26.6 us -> 26.1 us (0.981)
  Pallas kernels: 25.8 us -> 25.3 us
    pallas_call x1, Pallas kernels: 25 us -> 24.4 us  [on_device(): pl.pallas_call(functools.partial(kernel, n), out_shape=(pltpu.VMEM((parts...]
where the time goes in v3:
time: 26.1 us; the launch traced here: 25.9 us
  Pallas kernels  25.3 us (97%)
  between operations  0.66 us (3%)
    pallas_call x1, Pallas kernels, on_device(): pl.pallas_call(functools.partial(kernel, n), out_shape=(pltpu.VMEM((parts...  24.4 us
    pallas_call x1, Pallas kernels, on_device(): pl.pallas_call(functools.partial(finish, n), out_shape=(jax.ShapeDtypeStr...  0.82 us

profile of v3, /device:TPU:0, one launch (start us, length us, event | category | flops | bytes accessed | tf_op | source)
XLA Modules:
  0.0 25.9 jit_solution(6099859938651661483)
XLA Ops:
  0.6 0.0 copy-start
  0.6 24.4 %shard_map.102 = (f32[64,512]{1,0:T(8,128)S(1)}, f32[64,512]{1,0:T(8,128)S(1)}, f32[8,4,64]{2,1,0:T(4,128)S(1)}) custom-call(bf16[8,8448]{1,0:T(8,128)(2,1)} %particles.1, f32[1,8]{1,0:T(1,128)} %bitcast.7, f32[4224]{0:T(1024)} %noise_hbm.1, bf16[432,8448]{1,0:T(8,128)(2,1)} %references.1, s32[1,64]{1,0:T(1,128)} %bitcast.8, s32[1,64]{1,0:T(1,128)} %bitcast.9), custom_call_target="tpu_custom_call" | custom-call | tf_op jit(solution)/shard_map/pallas_call | solution.py:519
  25.1 0.0 copy-done
  25.1 0.8 %shard_map.103 = (f32[64,432]{1,0:T(8,128)}, f32[64,432]{1,0:T(8,128)}, f32[1,64]{1,0:T(1,128)}, f32[1,64]{1,0:T(1,128)}) custom-call(f32[64,512]{1,0:T(8,128)S(1)} %get-tuple-element.11.expon, f32[64,512]{1,0:T(8,128)S(1)} %get-tuple-element.12.prefix, f32[8,4,64]{2,1,0:T(4,128)S(1)} %get-tuple-element.13.sgath, s32[1,64]{1,0:T(1,128)S(1)} %bitcast.6), custom_call_target="tpu_custom_call" | custom-call | tf_op jit(solution)/shard_map/pallas_call | solution.py:561
Async XLA Ops:
  0.6 24.5 %copy-start = (s32[64]{0:T(128)S(1)}, s32[64]{0:T(128)}, u32[]{:S(2)}) copy-start(s32[64]{0:T(128)} %param.11) | copy-start | bytes 772

commit v4 on v3

--- a/solution.py
+++ b/solution.py
@@ -9,13 +9,12 @@
 from jax.sharding import PartitionSpec as P
 
 MESH = pl.DeviceIdType.MESH
-DIMS = (((1,), (1,)), ((), ()))
+SLAB = 384
 PIECES = 3
 SPANS = ((0, 4), (4, 6))
-EARLY = 1
-STEPS = ((0,), (1, 2), (3, 4, 5))
+BUDGET = (4, 2, 2, 1)
+STEPS = ((0,), (1, 2), (3, 4), (5,))
 ORDER = tuple(c for k in range(PIECES) for c in (k, k + PIECES))
-ROWS = 16
 
 
 def sin_of(x):
@@ -48,7 +47,7 @@
 def kernel(
     n, particles, defocus, noise_hbm, references, starts_hbm, lens_hbm,
     expon, prefix, sgath,
-    gath, dgath, refs, ctf, ctf_power, power, weighted, acc, mine, noise, starts, lens,
+    gath, dgath, refs, turned, ctf, ctf_power, power, weighted, acc, mine, noise, starts, lens,
     own_sem, piece_sem, ref_sem, up_send, down_send, side_send, recv, side_recv,
     dup_send, ddown_send, beside_send, beside_recv, pair_recv, far_send, far_recv, s_send, s_recv,
 ):
@@ -285,23 +284,36 @@
         def _():
             ctf_row(row + t)
 
-    def power_piece(k):
+    def loaded(k):
         both_parts = pl.ds(0, 2 * size)
         pltpu.make_async_copy(references.at[:, both_parts], refs.at[:, both_parts], ref_sem.at[k]).wait()
 
-        def body(i):
-            rows = pl.ds(pl.multiple_of(i * ROWS, ROWS), ROWS)
-            re = refs[rows, cut(k)].astype(jnp.float32)
-            im = refs[rows, cut(k + PIECES)].astype(jnp.float32)
-            power[rows, cut(k)] = (re * re + im * im).astype(jnp.bfloat16)
-
-        loop(ori // ROWS, body)
+    def turn_slab(start):
+        slab = pl.ds(start, SLAB)
+        twin = pl.ds(start + coef, SLAB)
+        re = refs[:, slab].T
+        im = refs[:, twin].T
+        turned[slab, :] = re
+        turned[twin, :] = im
+        re = re.astype(jnp.float32)
+        im = im.astype(jnp.float32)
+        power[slab, :] = (re * re + im * im).astype(jnp.bfloat16)
+
+    slabs = coef // SLAB
+    done = [0]
+
+    def slab_work(count):
+        for i in range(done[0], min(done[0] + count, slabs)):
+            for k in range(PIECES):
+                if i * SLAB <= k * size < (i + 1) * SLAB or (k and i * SLAB < k * size < (i + 1) * SLAB):
+                    loaded(k)
+            turn_slab(i * SLAB)
+        done[0] = min(done[0] + count, slabs)
 
     def energy():
         total = 0.0
         for k in range(PIECES):
-            total = total + lax.dot_general(
-                ctf_power[:, cut(k)], power[:, cut(k)], DIMS, preferred_element_type=jnp.float32)
+            total = total + jnp.dot(ctf_power[:, cut(k)], power[cut(k), :], preferred_element_type=jnp.float32)
         acc[...] = -0.5 * total
 
     def cross(pieces):
@@ -315,14 +327,20 @@
                 weighted[rows, cut(c)] = (raw * ctf[rows, cut(k)] * noise[cut(k)].reshape(1, size)).astype(jnp.bfloat16)
 
             loop(deep, body)
-            total = total + lax.dot_general(
-                weighted[:, cut(c)], refs[:, cut(c)], DIMS, preferred_element_type=jnp.float32)
+            total = total + jnp.dot(weighted[:, cut(c)], turned[cut(c), :], preferred_element_type=jnp.float32)
         acc[...] = total
 
-    for k in range(PIECES):
-        power_piece(k)
-        if k == EARLY:
-            relay_pairs(0)
+    if not short:
+        def slab_step(i, carry):
+            turn_slab(pl.multiple_of(i * SLAB, SLAB))
+            return carry
+
+        for k in range(PIECES):
+            loaded(k)
+        lax.fori_loop(0, slabs, slab_step, 0)
+    slab_work(BUDGET[0] if short else 0)
+    relay_pairs(0)
+    slab_work(BUDGET[1] if short else 0)
     for copy in small:
         copy.wait()
     if short:
@@ -333,6 +351,7 @@
             if c > 0:
                 fall(c - 1, 1)
 
+        slab_work(BUDGET[2])
         ctf_row(row)
 
         @pl.when(middle)
@@ -350,16 +369,12 @@
             relay_pairs(1)
             ctf_row(row - 1)
 
+        slab_work(BUDGET[3])
         for c in order:
             handle(c, 2)
-            if c == 3:
-                @pl.when(row == deep - 2)
-                def _():
-                    relay_pairs(2)
-
-        @pl.when(row != deep - 2)
-        def _():
-            relay_pairs(2)
+            if c in (2, 4):
+                slab_work(1)
+        relay_pairs(2)
 
         @pl.when(middle)
         def _():
@@ -367,6 +382,10 @@
             ctf_row(row + 1)
             ctf_rows(2)
 
+        @pl.when(highest)
+        def _():
+            ctf_rows(2)
+
         @pl.when(lowest)
         def _():
             ctf_rows(2)
@@ -375,22 +394,19 @@
 
         for c in order:
             handle(c, 3)
-            if c == 1:
-                @pl.when(highest)
-                def _():
-                    ctf_rows(2)
-
-            if c == 3:
-                @pl.when(highest)
-                def _():
-                    relay_pairs(3)
-                    ctf_rows(3)
+        @pl.when(highest)
+        def _():
+            relay_pairs(3)
+            ctf_rows(3)
+
     else:
         for t in range(1, deep):
             relay_pairs(t)
             for c in order:
                 handle(c, t)
         loop(deep, ctf_row)
+    if short:
+        slab_work(slabs)
     energy()
     for step in STEPS if short else [(c,) for c in order]:
         for c in step:
@@ -529,9 +545,10 @@
             pltpu.VMEM((n, per, feat), bf16),
             pltpu.VMEM((n, 1, per), f32),
             pltpu.VMEM((ori, feat), bf16),
+            pltpu.VMEM((feat, ori), bf16),
             pltpu.VMEM((parts, coef), f32),
             pltpu.VMEM((parts, coef), bf16),
-            pltpu.VMEM((ori, coef), bf16),
+            pltpu.VMEM((coef, ori), bf16),
             pltpu.VMEM((parts, feat), bf16),
             pltpu.VMEM((parts, ori), f32),
             pltpu.VMEM((4, parts), f32),
@@ -551,7 +568,7 @@
             dma, dma,
         ],
         compiler_params=pltpu.CompilerParams(
-            collective_id=0, has_side_effects=True, vmem_limit_bytes=48 * 1024 * 1024
+            collective_id=0, has_side_effects=True, vmem_limit_bytes=56 * 1024 * 1024
         ),
     )(*(
         pltpu.with_memory_space_constraint(x, pltpu.HBM) for x in (

time: 26.1 us -> 24.9 us (0.954)
  Pallas kernels: 25.3 us -> 24 us
    pallas_call x1, Pallas kernels: 24.4 us -> 23.2 us  [on_device(): pl.pallas_call(functools.partial(kernel, n), out_shape=(pltpu.VMEM((parts...]
where the time goes in v4:
time: 24.9 us; the launch traced here: 24.7 us
  Pallas kernels  24 us (96%)
  between operations  0.66 us (3%)
    pallas_call x1, Pallas kernels, on_device(): pl.pallas_call(functools.partial(kernel, n), out_shape=(pltpu.VMEM((parts...  23.2 us
    pallas_call x1, Pallas kernels, on_device(): pl.pallas_call(functools.partial(finish, n), out_shape=(jax.ShapeDtypeStr...  0.82 us

profile of v4, /device:TPU:0, one launch (start us, length us, event | category | flops | bytes accessed | tf_op | source)
XLA Modules:
  0.0 24.7 jit_solution(12665553501362696580)
XLA Ops:
  0.6 0.0 copy-start
  0.6 23.2 %shard_map.102 = (f32[64,512]{1,0:T(8,128)S(1)}, f32[64,512]{1,0:T(8,128)S(1)}, f32[8,4,64]{2,1,0:T(4,128)S(1)}) custom-call(bf16[8,8448]{1,0:T(8,128)(2,1)} %particles.1, f32[1,8]{1,0:T(1,128)} %bitcast.7, f32[4224]{0:T(1024)} %noise_hbm.1, bf16[432,8448]{1,0:T(8,128)(2,1)} %references.1, s32[1,64]{1,0:T(1,128)} %bitcast.8, s32[1,64]{1,0:T(1,128)} %bitcast.9), custom_call_target="tpu_custom_call" | custom-call | tf_op jit(solution)/shard_map/pallas_call | solution.py:535
  23.9 0.0 copy-done
  23.9 0.8 %shard_map.103 = (f32[64,432]{1,0:T(8,128)}, f32[64,432]{1,0:T(8,128)}, f32[1,64]{1,0:T(1,128)}, f32[1,64]{1,0:T(1,128)}) custom-call(f32[64,512]{1,0:T(8,128)S(1)} %get-tuple-element.11.expon, f32[64,512]{1,0:T(8,128)S(1)} %get-tuple-element.12.prefix, f32[8,4,64]{2,1,0:T(4,128)S(1)} %get-tuple-element.13.sgath, s32[1,64]{1,0:T(1,128)S(1)} %bitcast.6), custom_call_target="tpu_custom_call" | custom-call | tf_op jit(solution)/shard_map/pallas_call | solution.py:578
Async XLA Ops:
  0.6 23.2 %copy-start = (s32[64]{0:T(128)S(1)}, s32[64]{0:T(128)}, u32[]{:S(2)}) copy-start(s32[64]{0:T(128)} %param.11) | copy-start | bytes 772

commit v5 on v4

--- a/solution.py
+++ b/solution.py
@@ -12,8 +12,8 @@
 SLAB = 384
 PIECES = 3
 SPANS = ((0, 4), (4, 6))
-BUDGET = (4, 2, 2, 1)
-STEPS = ((0,), (1, 2), (3, 4), (5,))
+BOUNDS = (3, 5, 7, 8, 9, 10)
+STEPS = ((0, 1), (2, 3), (4, 5))
 ORDER = tuple(c for k in range(PIECES) for c in (k, k + PIECES))
 
 
@@ -269,8 +269,9 @@
             col_pos = ((index & 127) - 64).astype(jnp.float32)
             freq = math.pi * (row_pos * row_pos + col_pos * col_pos) / 16384.0
             value = -sin_of(d * freq + 0.07)
-            ctf[rows, cut(k)] = value
-            ctf_power[rows, cut(k)] = (value * value * noise[cut(k)].reshape(1, size)).astype(jnp.bfloat16)
+            inverse = noise[cut(k)].reshape(1, size)
+            ctf[rows, cut(k)] = value * inverse
+            ctf_power[rows, cut(k)] = (value * value * inverse).astype(jnp.bfloat16)
 
         for k in range(PIECES):
             body(k)
@@ -300,15 +301,16 @@
         power[slab, :] = (re * re + im * im).astype(jnp.bfloat16)
 
     slabs = coef // SLAB
-    done = [0]
-
-    def slab_work(count):
-        for i in range(done[0], min(done[0] + count, slabs)):
+    def turn_slabs(first, last):
+        for i in range(first, min(last, slabs)):
+            turn_slab(i * SLAB)
+
+    def slab_work(first, last):
+        for i in range(first, min(last, slabs)):
             for k in range(PIECES):
-                if i * SLAB <= k * size < (i + 1) * SLAB or (k and i * SLAB < k * size < (i + 1) * SLAB):
+                if i * SLAB <= k * size < (i + 1) * SLAB:
                     loaded(k)
             turn_slab(i * SLAB)
-        done[0] = min(done[0] + count, slabs)
 
     def energy():
         total = 0.0
@@ -324,7 +326,7 @@
             def body(i):
                 rows = pl.ds(pl.multiple_of(i * group, group), group)
                 raw = gath[pl.ds(i * wide, wide), :, cut(c)].astype(jnp.float32).reshape(group, size)
-                weighted[rows, cut(c)] = (raw * ctf[rows, cut(k)] * noise[cut(k)].reshape(1, size)).astype(jnp.bfloat16)
+                weighted[rows, cut(c)] = (raw * ctf[rows, cut(k)]).astype(jnp.bfloat16)
 
             loop(deep, body)
             total = total + jnp.dot(weighted[:, cut(c)], turned[cut(c), :], preferred_element_type=jnp.float32)
@@ -338,9 +340,11 @@
         for k in range(PIECES):
             loaded(k)
         lax.fori_loop(0, slabs, slab_step, 0)
-    slab_work(BUDGET[0] if short else 0)
+    if short:
+        slab_work(0, BOUNDS[0])
     relay_pairs(0)
-    slab_work(BUDGET[1] if short else 0)
+    if short:
+        slab_work(BOUNDS[0], BOUNDS[1])
     for copy in small:
         copy.wait()
     if short:
@@ -351,12 +355,15 @@
             if c > 0:
                 fall(c - 1, 1)
 
-        slab_work(BUDGET[2])
+        @pl.when(middle)
+        def _():
+            relay_pairs(1)
+
+        @pl.when(jnp.logical_not(middle))
+        def _():
+            turn_slabs(BOUNDS[1], BOUNDS[2])
+
         ctf_row(row)
-
-        @pl.when(middle)
-        def _():
-            relay_pairs(1)
 
 
         @pl.when(lowest)
@@ -369,12 +376,37 @@
             relay_pairs(1)
             ctf_row(row - 1)
 
-        slab_work(BUDGET[3])
+        @pl.when(jnp.logical_not(middle))
+        def _():
+            for k in range(PIECES):
+                if BOUNDS[2] * SLAB <= k * size:
+                    loaded(k)
+            turn_slabs(BOUNDS[2], BOUNDS[3])
+
         for c in order:
             handle(c, 2)
             if c in (2, 4):
-                slab_work(1)
-        relay_pairs(2)
+                @pl.when(jnp.logical_not(middle))
+                def _():
+                    turn_slabs(BOUNDS[1 + c // 2 + 1], BOUNDS[1 + c // 2 + 2])
+
+        @pl.when(jnp.logical_not(middle))
+        def _():
+            turn_slabs(BOUNDS[5], slabs)
+
+        @pl.when(row == deep - 2)
+        def _():
+            relay_pairs(2)
+
+        @pl.when(middle)
+        def _():
+            for k in range(PIECES):
+                if BOUNDS[2] * SLAB <= k * size:
+                    loaded(k)
+            turn_slabs(BOUNDS[1], slabs)
+        @pl.when(row != deep - 2)
+        def _():
+            relay_pairs(2)
 
         @pl.when(middle)
         def _():
@@ -405,8 +437,6 @@
             for c in order:
                 handle(c, t)
         loop(deep, ctf_row)
-    if short:
-        slab_work(slabs)
     energy()
     for step in STEPS if short else [(c,) for c in order]:
         for c in step:

time: 24.9 us -> 24.8 us (level)
  no operation moved by 1% of the time
where the time goes in v5:
time: 24.8 us; the launch traced here: 24.7 us
  Pallas kernels  24 us (97%)
  between operations  0.66 us (3%)
    pallas_call x1, Pallas kernels, on_device(): pl.pallas_call(functools.partial(kernel, n), out_shape=(pltpu.VMEM((parts...  23.2 us
    pallas_call x1, Pallas kernels, on_device(): pl.pallas_call(functools.partial(finish, n), out_shape=(jax.ShapeDtypeStr...  0.82 us

profile of v5, /device:TPU:0, one launch (start us, length us, event | category | flops | bytes accessed | tf_op | source)
XLA Modules:
  0.0 24.7 jit_solution(8659893310641712609)
XLA Ops:
  0.6 0.0 copy-start
  0.6 23.2 %shard_map.102 = (f32[64,512]{1,0:T(8,128)S(1)}, f32[64,512]{1,0:T(8,128)S(1)}, f32[8,4,64]{2,1,0:T(4,128)S(1)}) custom-call(bf16[8,8448]{1,0:T(8,128)(2,1)} %particles.1, f32[1,8]{1,0:T(1,128)} %bitcast.7, f32[4224]{0:T(1024)} %noise_hbm.1, bf16[432,8448]{1,0:T(8,128)(2,1)} %references.1, s32[1,64]{1,0:T(1,128)} %bitcast.8, s32[1,64]{1,0:T(1,128)} %bitcast.9), custom_call_target="tpu_custom_call" | custom-call | tf_op jit(solution)/shard_map/pallas_call | solution.py:565
  23.8 0.0 copy-done
  23.8 0.8 %shard_map.103 = (f32[64,432]{1,0:T(8,128)}, f32[64,432]{1,0:T(8,128)}, f32[1,64]{1,0:T(1,128)}, f32[1,64]{1,0:T(1,128)}) custom-call(f32[64,512]{1,0:T(8,128)S(1)} %get-tuple-element.11.expon, f32[64,512]{1,0:T(8,128)S(1)} %get-tuple-element.12.prefix, f32[8,4,64]{2,1,0:T(4,128)S(1)} %get-tuple-element.13.sgath, s32[1,64]{1,0:T(1,128)S(1)} %bitcast.6), custom_call_target="tpu_custom_call" | custom-call | tf_op jit(solution)/shard_map/pallas_call | solution.py:608
Async XLA Ops:
  0.6 23.2 %copy-start = (s32[64]{0:T(128)S(1)}, s32[64]{0:T(128)}, u32[]{:S(2)}) copy-start(s32[64]{0:T(128)} %param.11) | copy-start | bytes 772

commit v6 on v5

--- a/solution.py
+++ b/solution.py
@@ -13,7 +13,7 @@
 PIECES = 3
 SPANS = ((0, 4), (4, 6))
 BOUNDS = (3, 5, 7, 8, 9, 10)
-STEPS = ((0, 1), (2, 3), (4, 5))
+STEPS = ((0,), (1, 2), (3, 4, 5))
 ORDER = tuple(c for k in range(PIECES) for c in (k, k + PIECES))
 
 

time: 24.8 us -> 24.8 us (level)
  no operation moved by 1% of the time
where the time goes in v6:
time: 24.8 us; the launch traced here: 24.6 us
  Pallas kernels  24 us (97%)
  between operations  0.66 us (3%)
    pallas_call x1, Pallas kernels, on_device(): pl.pallas_call(functools.partial(kernel, n), out_shape=(pltpu.VMEM((parts...  23.2 us
    pallas_call x1, Pallas kernels, on_device(): pl.pallas_call(functools.partial(finish, n), out_shape=(jax.ShapeDtypeStr...  0.82 us

profile of v6, /device:TPU:0, one launch (start us, length us, event | category | flops | bytes accessed | tf_op | source)
XLA Modules:
  0.0 24.6 jit_solution(11271831711413818277)
XLA Ops:
  0.6 0.0 copy-start
  0.6 23.2 %shard_map.102 = (f32[64,512]{1,0:T(8,128)S(1)}, f32[64,512]{1,0:T(8,128)S(1)}, f32[8,4,64]{2,1,0:T(4,128)S(1)}) custom-call(bf16[8,8448]{1,0:T(8,128)(2,1)} %particles.1, f32[1,8]{1,0:T(1,128)} %bitcast.7, f32[4224]{0:T(1024)} %noise_hbm.1, bf16[432,8448]{1,0:T(8,128)(2,1)} %references.1, s32[1,64]{1,0:T(1,128)} %bitcast.8, s32[1,64]{1,0:T(1,128)} %bitcast.9), custom_call_target="tpu_custom_call" | custom-call | tf_op jit(solution)/shard_map/pallas_call | solution.py:565
  23.8 0.0 copy-done
  23.8 0.8 %shard_map.103 = (f32[64,432]{1,0:T(8,128)}, f32[64,432]{1,0:T(8,128)}, f32[1,64]{1,0:T(1,128)}, f32[1,64]{1,0:T(1,128)}) custom-call(f32[64,512]{1,0:T(8,128)S(1)} %get-tuple-element.11.expon, f32[64,512]{1,0:T(8,128)S(1)} %get-tuple-element.12.prefix, f32[8,4,64]{2,1,0:T(4,128)S(1)} %get-tuple-element.13.sgath, s32[1,64]{1,0:T(1,128)S(1)} %bitcast.6), custom_call_target="tpu_custom_call" | custom-call | tf_op jit(solution)/shard_map/pallas_call | solution.py:608
Async XLA Ops:
  0.6 23.2 %copy-start = (s32[64]{0:T(128)S(1)}, s32[64]{0:T(128)}, u32[]{:S(2)}) copy-start(s32[64]{0:T(128)} %param.11) | copy-start | bytes 772
